TPU v7x, 128 devices: a whole 4x4x4 slice. The times are simulated.
128 devices in a mesh: sec: 64 (over x, y, z), node: 2 (over core).
Axes of the slice: x: 4, y: 4, z: 4, core: 2. Of those that a mesh axis runs over, the one named last changes fastest.
Arguments:
- env_blocks: bfloat16 [2, 24576, 128, 128], P('node', 'sec'), may hold values from -10 to 10, as said below
- iso_blocks: bfloat16 [2, 24576, 128, 128], P('node', 'sec'), may hold values from -6 to 6
- joined_sector: int32 [2, 24576], P('node', 'sec'), may hold values from 0 to 63, as said below
- owner_map: int32 [2, 64], P('node'), may hold values from 0 to 63, each once within a row
- live_pairs: int32 [2, 64], P('node', 'sec'), may hold values from 1 to 384, as said below
Outputs:
- environment: float32 [2, 64, 128, 128], P('node', 'sec')
Inputs may be any that keep to these rules, and one draw needn't show every extreme that they name: `env_blocks`: each block is symmetric. `joined_sector`: slot p belongs to tree node k = p // 3072 of its group, and its sector is one of that node's sectors k * 8 to k * 8 + 7. `owner_map`: each row names every index once. `live_pairs`: in every group some index of sec has all 384 slots live.
All inputs are finite; a program needn't handle non-finite values.
Results may differ from a plain program's by a relative error of at most 0.0003.
Values sent between devices are 32-bit elements; how exact they have to be, the bound alone decides.
A program may use at most 128 MiB of HBM per device.

v0:
```python
import jax
import jax.numpy as jnp
from jax import lax
from jax.sharding import Mesh
from jax.sharding import PartitionSpec as P

SEC = ("sec_0", "sec_1", "sec_2")
SEC_NODE = ("sec_0", "sec_1", "sec_2", "node")
pair_group = 32


def cut_along(shard, dim, length):
    shape = shard.shape
    blocks = shard.reshape(*shape[:dim], length, shape[dim] // length, *shape[dim + 1 :])
    return jnp.moveaxis(blocks, dim, 0)


def sum_at_owner(shard, axis, dim):
    length = lax.axis_size(axis)
    blocks = lax.all_to_all(cut_along(shard, dim, length), axis, 0, 0, tiled=True)
    return jnp.sum(blocks, axis=0)


def by_axis(shard, axes):
    for axis in axes:
        shard = lax.psum(shard, axis)
    return shard


def body(env_blocks, iso_blocks, joined_sector, owner_map, live_pairs):
    pairs_here = env_blocks.shape[1]
    sector_width = iso_blocks.shape[3]
    half_width = sector_width // 2
    sectors = lax.axis_size(SEC)
    sector_ids = jnp.arange(sectors, dtype=jnp.int32)
    matches = joined_sector[0][:, None] == sector_ids[None, :]
    targets = jnp.sum(jnp.where(matches, owner_map[0][None, :], 0), axis=1)
    living = jnp.arange(pairs_here, dtype=jnp.int32) < live_pairs[0, 0]

    def add_group(turn_index, partial_value):
        first_pair = turn_index * pair_group
        blocks = lax.dynamic_slice_in_dim(env_blocks[0], first_pair, pair_group, 0)
        weights = lax.dynamic_slice_in_dim(iso_blocks[0], first_pair, pair_group, 0)
        group_targets = lax.dynamic_slice_in_dim(targets, first_pair, pair_group, 0)
        group_live = lax.dynamic_slice_in_dim(living, first_pair, pair_group, 0)
        product = jnp.einsum(
            "prk,pkc->prc", blocks, weights, preferred_element_type=jnp.float32
        ).astype(jnp.bfloat16)
        sandwich = jnp.einsum("prc,prd->pcd", weights, product, preferred_element_type=jnp.float32)
        selector = ((group_targets[:, None] == sector_ids[None, :]) & group_live[:, None]).astype(
            jnp.float32
        )
        flat_terms = sandwich.reshape(pair_group, sector_width * sector_width)
        added = lax.dot_general(
            selector,
            flat_terms,
            (((0,), (0,)), ((), ())),
            precision=lax.Precision.HIGHEST,
            preferred_element_type=jnp.float32,
        )
        return partial_value + added

    zero_sums = jnp.zeros((sectors, sector_width * sector_width), jnp.float32)
    turn_total = pairs_here // pair_group
    partial_value = lax.fori_loop(0, turn_total, add_group, zero_sums).reshape(
        sectors, sector_width, sector_width
    )
    upper_left = partial_value[:, :half_width, :half_width]
    upper_right = partial_value[:, :half_width, half_width:]
    lower_right = partial_value[:, half_width:, half_width:]
    corners = jnp.triu(upper_left) + jnp.tril(jnp.swapaxes(lower_right, 1, 2), -1)
    diagonal_row = jnp.diagonal(lower_right, axis1=1, axis2=2)[:, None, :]
    packed = jnp.concatenate((corners, upper_right, diagonal_row), axis=1)
    summed = sum_at_owner(packed, SEC, 0)[0]
    corners_sum = summed[:half_width]
    right_sum = summed[half_width : 2 * half_width]
    diagonal_sum = summed[2 * half_width]
    left_block = jnp.triu(corners_sum) + jnp.triu(corners_sum, 1).T
    lower_upper = jnp.tril(corners_sum, -1).T + jnp.diag(diagonal_sum)
    right_block = lower_upper + jnp.triu(lower_upper, 1).T
    top_rows = jnp.concatenate((left_block, right_sum), axis=1)
    bottom_rows = jnp.concatenate((right_sum.T, right_block), axis=1)
    hermitian = jnp.concatenate((top_rows, bottom_rows), axis=0)
    squares = jnp.sum(hermitian * hermitian)
    grand_total = by_axis(squares, SEC_NODE)
    entries = sectors * lax.axis_size("node") * sector_width * sector_width
    factor = lax.rsqrt(grand_total / entries + 1e-06)
    return (hermitian * factor)[None, None]


def solution(mesh):
    split = Mesh(
        mesh.devices.reshape(4, 4, 4, mesh.shape["node"]), ("sec_0", "sec_1", "sec_2", "node")
    )
    placed = (
        P("node", SEC, None, None),
        P("node", SEC, None, None),
        P("node", SEC),
        P("node", None),
        P("node", SEC),
    )
    return jax.shard_map(
        body, mesh=split, in_specs=placed, out_specs=P("node", SEC, None, None), check_vma=False
    )
```

profile of v0, /device:TPU:1, one launch (start us, length us, event | category | flops | bytes accessed | tf_op | source)
XLA Modules:
  0.0 255.1 jit_solution(2081290549324022647)
XLA Ops:
  0.0 0.7 reduce.1
  1.4 0.7 select_reduce_fusion
  2.1 121.4 %while.14 = (s32[]{:T(128)}, f32[64,16384]{1,0:T(8,128)}, s32[384]{0:T(512)S(1)}, pred[384]{0:T(512)(128)(4,1)S(1)}, bf16[1,384,128,128]{3,2,1,0:T(8,128)(2,1)},...) while((s32[]{:T(128)}, f32[64,16384]{1,0:T(8,128)}, ...), condition=%wide.region_2.3_spmd.clone, body=%wide.region_1.2_spmd.clone.sunk | while | flops 673714176 | bytes 15730821 | solution.py:65
  2.1 2.6 %fusion.36 = f32[32,128,128]{2,1,0:T(8,128)S(1)} fusion(bf16[1,384,128,128]{3,2,1,0:T(8,128)(2,1)} %get-tuple-element.248, s32[]{:T(128)S(6)} %select_n.72, bf16[1,384,128,128]{3,2,1,0:T(8,128)(2,1)} %get-tuple-element.247), kind=kOutput, calls=%fused_computation.6.clone.1 | convolution fusion | flops 268959744 | bytes 5244416 | tf_op jit(solution)/shard_map/while/body/eval_jaxpr/prc,prd->pcd/dot_general | solution.py:49
  4.8 0.1 dynamic_slice.54
  4.8 0.1 dynamic_slice.55
  4.9 5.3 %convolution_add_fusion.2 = f32[64,16384]{1,0:T(8,128)} fusion(f32[64,16384]{1,0:T(8,128)} %get-tuple-element.234, f32[4,8,128,128]{3,2,1,0:T(8,128)S(1)} %bitcast.64, pred[]{:T(512)S(6)} %compare.3, s32[32]{0:T(128)S(1)} %dynamic_slice.54, pred[32]{0:T(512)(128)(4,1)S(1)} %dynamic_slice.55), kind=kOutput, calls=%fused_computation.2.clone.1 | convolution fusion | flops 404754432 | bytes 10485921 | tf_op jit(solution)/shard_map/while/body/eval_jaxpr/dot_general | solution.py:54
  10.2 2.6 %fusion.36 = f32[32,128,128]{2,1,0:T(8,128)S(1)} fusion(bf16[1,384,128,128]{3,2,1,0:T(8,128)(2,1)} %get-tuple-element.248, s32[]{:T(128)S(6)} %select_n.72, bf16[1,384,128,128]{3,2,1,0:T(8,128)(2,1)} %get-tuple-element.247), kind=kOutput, calls=%fused_computation.6.clone.1 | convolution fusion | flops 268959744 | bytes 5244416 | tf_op jit(solution)/shard_map/while/body/eval_jaxpr/prc,prd->pcd/dot_general | solution.py:49
  12.8 0.1 dynamic_slice.54
  13.0 7.5 %convolution_add_fusion.2 = f32[64,16384]{1,0:T(8,128)} fusion(f32[64,16384]{1,0:T(8,128)} %get-tuple-element.234, f32[4,8,128,128]{3,2,1,0:T(8,128)S(1)} %bitcast.64, pred[]{:T(512)S(6)} %compare.3, s32[32]{0:T(128)S(1)} %dynamic_slice.54, pred[32]{0:T(512)(128)(4,1)S(1)} %dynamic_slice.55), kind=kOutput, calls=%fused_computation.2.clone.1 | convolution fusion | flops 404754432 | bytes 10485921 | tf_op jit(solution)/shard_map/while/body/eval_jaxpr/dot_general | solution.py:54
  20.5 2.6 %fusion.36 = f32[32,128,128]{2,1,0:T(8,128)S(1)} fusion(bf16[1,384,128,128]{3,2,1,0:T(8,128)(2,1)} %get-tuple-element.248, s32[]{:T(128)S(6)} %select_n.72, bf16[1,384,128,128]{3,2,1,0:T(8,128)(2,1)} %get-tuple-element.247), kind=kOutput, calls=%fused_computation.6.clone.1 | convolution fusion | flops 268959744 | bytes 5244416 | tf_op jit(solution)/shard_map/while/body/eval_jaxpr/prc,prd->pcd/dot_general | solution.py:49
  23.1 0.1 dynamic_slice.54
  23.2 0.1 dynamic_slice.55
  23.3 7.5 %convolution_add_fusion.2 = f32[64,16384]{1,0:T(8,128)} fusion(f32[64,16384]{1,0:T(8,128)} %get-tuple-element.234, f32[4,8,128,128]{3,2,1,0:T(8,128)S(1)} %bitcast.64, pred[]{:T(512)S(6)} %compare.3, s32[32]{0:T(128)S(1)} %dynamic_slice.54, pred[32]{0:T(512)(128)(4,1)S(1)} %dynamic_slice.55), kind=kOutput, calls=%fused_computation.2.clone.1 | convolution fusion | flops 404754432 | bytes 10485921 | tf_op jit(solution)/shard_map/while/body/eval_jaxpr/dot_general | solution.py:54
  30.8 2.6 %fusion.36 = f32[32,128,128]{2,1,0:T(8,128)S(1)} fusion(bf16[1,384,128,128]{3,2,1,0:T(8,128)(2,1)} %get-tuple-element.248, s32[]{:T(128)S(6)} %select_n.72, bf16[1,384,128,128]{3,2,1,0:T(8,128)(2,1)} %get-tuple-element.247), kind=kOutput, calls=%fused_computation.6.clone.1 | convolution fusion | flops 268959744 | bytes 5244416 | tf_op jit(solution)/shard_map/while/body/eval_jaxpr/prc,prd->pcd/dot_general | solution.py:49
  33.4 0.1 dynamic_slice.54
  33.5 7.5 %convolution_add_fusion.2 = f32[64,16384]{1,0:T(8,128)} fusion(f32[64,16384]{1,0:T(8,128)} %get-tuple-element.234, f32[4,8,128,128]{3,2,1,0:T(8,128)S(1)} %bitcast.64, pred[]{:T(512)S(6)} %compare.3, s32[32]{0:T(128)S(1)} %dynamic_slice.54, pred[32]{0:T(512)(128)(4,1)S(1)} %dynamic_slice.55), kind=kOutput, calls=%fused_computation.2.clone.1 | convolution fusion | flops 404754432 | bytes 10485921 | tf_op jit(solution)/shard_map/while/body/eval_jaxpr/dot_general | solution.py:54
  41.0 2.6 %fusion.36 = f32[32,128,128]{2,1,0:T(8,128)S(1)} fusion(bf16[1,384,128,128]{3,2,1,0:T(8,128)(2,1)} %get-tuple-element.248, s32[]{:T(128)S(6)} %select_n.72, bf16[1,384,128,128]{3,2,1,0:T(8,128)(2,1)} %get-tuple-element.247), kind=kOutput, calls=%fused_computation.6.clone.1 | convolution fusion | flops 268959744 | bytes 5244416 | tf_op jit(solution)/shard_map/while/body/eval_jaxpr/prc,prd->pcd/dot_general | solution.py:49
  43.7 0.1 dynamic_slice.54
  43.8 7.5 %convolution_add_fusion.2 = f32[64,16384]{1,0:T(8,128)} fusion(f32[64,16384]{1,0:T(8,128)} %get-tuple-element.234, f32[4,8,128,128]{3,2,1,0:T(8,128)S(1)} %bitcast.64, pred[]{:T(512)S(6)} %compare.3, s32[32]{0:T(128)S(1)} %dynamic_slice.54, pred[32]{0:T(512)(128)(4,1)S(1)} %dynamic_slice.55), kind=kOutput, calls=%fused_computation.2.clone.1 | convolution fusion | flops 404754432 | bytes 10485921 | tf_op jit(solution)/shard_map/while/body/eval_jaxpr/dot_general | solution.py:54
  51.3 2.6 %fusion.36 = f32[32,128,128]{2,1,0:T(8,128)S(1)} fusion(bf16[1,384,128,128]{3,2,1,0:T(8,128)(2,1)} %get-tuple-element.248, s32[]{:T(128)S(6)} %select_n.72, bf16[1,384,128,128]{3,2,1,0:T(8,128)(2,1)} %get-tuple-element.247), kind=kOutput, calls=%fused_computation.6.clone.1 | convolution fusion | flops 268959744 | bytes 5244416 | tf_op jit(solution)/shard_map/while/body/eval_jaxpr/prc,prd->pcd/dot_general | solution.py:49
  54.0 0.1 dynamic_slice.54
  54.1 7.5 %convolution_add_fusion.2 = f32[64,16384]{1,0:T(8,128)} fusion(f32[64,16384]{1,0:T(8,128)} %get-tuple-element.234, f32[4,8,128,128]{3,2,1,0:T(8,128)S(1)} %bitcast.64, pred[]{:T(512)S(6)} %compare.3, s32[32]{0:T(128)S(1)} %dynamic_slice.54, pred[32]{0:T(512)(128)(4,1)S(1)} %dynamic_slice.55), kind=kOutput, calls=%fused_computation.2.clone.1 | convolution fusion | flops 404754432 | bytes 10485921 | tf_op jit(solution)/shard_map/while/body/eval_jaxpr/dot_general | solution.py:54
  61.6 2.8 %fusion.36 = f32[32,128,128]{2,1,0:T(8,128)S(1)} fusion(bf16[1,384,128,128]{3,2,1,0:T(8,128)(2,1)} %get-tuple-element.248, s32[]{:T(128)S(6)} %select_n.72, bf16[1,384,128,128]{3,2,1,0:T(8,128)(2,1)} %get-tuple-element.247), kind=kOutput, calls=%fused_computation.6.clone.1 | convolution fusion | flops 268959744 | bytes 5244416 | tf_op jit(solution)/shard_map/while/body/eval_jaxpr/prc,prd->pcd/dot_general | solution.py:49
  64.4 0.1 dynamic_slice.54
  64.6 7.5 %convolution_add_fusion.2 = f32[64,16384]{1,0:T(8,128)} fusion(f32[64,16384]{1,0:T(8,128)} %get-tuple-element.234, f32[4,8,128,128]{3,2,1,0:T(8,128)S(1)} %bitcast.64, pred[]{:T(512)S(6)} %compare.3, s32[32]{0:T(128)S(1)} %dynamic_slice.54, pred[32]{0:T(512)(128)(4,1)S(1)} %dynamic_slice.55), kind=kOutput, calls=%fused_computation.2.clone.1 | convolution fusion | flops 404754432 | bytes 10485921 | tf_op jit(solution)/shard_map/while/body/eval_jaxpr/dot_general | solution.py:54
  72.1 2.6 %fusion.36 = f32[32,128,128]{2,1,0:T(8,128)S(1)} fusion(bf16[1,384,128,128]{3,2,1,0:T(8,128)(2,1)} %get-tuple-element.248, s32[]{:T(128)S(6)} %select_n.72, bf16[1,384,128,128]{3,2,1,0:T(8,128)(2,1)} %get-tuple-element.247), kind=kOutput, calls=%fused_computation.6.clone.1 | convolution fusion | flops 268959744 | bytes 5244416 | tf_op jit(solution)/shard_map/while/body/eval_jaxpr/prc,prd->pcd/dot_general | solution.py:49
  74.7 0.1 dynamic_slice.54
  74.9 7.5 %convolution_add_fusion.2 = f32[64,16384]{1,0:T(8,128)} fusion(f32[64,16384]{1,0:T(8,128)} %get-tuple-element.234, f32[4,8,128,128]{3,2,1,0:T(8,128)S(1)} %bitcast.64, pred[]{:T(512)S(6)} %compare.3, s32[32]{0:T(128)S(1)} %dynamic_slice.54, pred[32]{0:T(512)(128)(4,1)S(1)} %dynamic_slice.55), kind=kOutput, calls=%fused_computation.2.clone.1 | convolution fusion | flops 404754432 | bytes 10485921 | tf_op jit(solution)/shard_map/while/body/eval_jaxpr/dot_general | solution.py:54
  82.4 2.6 %fusion.36 = f32[32,128,128]{2,1,0:T(8,128)S(1)} fusion(bf16[1,384,128,128]{3,2,1,0:T(8,128)(2,1)} %get-tuple-element.248, s32[]{:T(128)S(6)} %select_n.72, bf16[1,384,128,128]{3,2,1,0:T(8,128)(2,1)} %get-tuple-element.247), kind=kOutput, calls=%fused_computation.6.clone.1 | convolution fusion | flops 268959744 | bytes 5244416 | tf_op jit(solution)/shard_map/while/body/eval_jaxpr/prc,prd->pcd/dot_general | solution.py:49
  85.0 0.1 dynamic_slice.54
  85.2 7.5 %convolution_add_fusion.2 = f32[64,16384]{1,0:T(8,128)} fusion(f32[64,16384]{1,0:T(8,128)} %get-tuple-element.234, f32[4,8,128,128]{3,2,1,0:T(8,128)S(1)} %bitcast.64, pred[]{:T(512)S(6)} %compare.3, s32[32]{0:T(128)S(1)} %dynamic_slice.54, pred[32]{0:T(512)(128)(4,1)S(1)} %dynamic_slice.55), kind=kOutput, calls=%fused_computation.2.clone.1 | convolution fusion | flops 404754432 | bytes 10485921 | tf_op jit(solution)/shard_map/while/body/eval_jaxpr/dot_general | solution.py:54
  92.7 2.6 %fusion.36 = f32[32,128,128]{2,1,0:T(8,128)S(1)} fusion(bf16[1,384,128,128]{3,2,1,0:T(8,128)(2,1)} %get-tuple-element.248, s32[]{:T(128)S(6)} %select_n.72, bf16[1,384,128,128]{3,2,1,0:T(8,128)(2,1)} %get-tuple-element.247), kind=kOutput, calls=%fused_computation.6.clone.1 | convolution fusion | flops 268959744 | bytes 5244416 | tf_op jit(solution)/shard_map/while/body/eval_jaxpr/prc,prd->pcd/dot_general | solution.py:49
  95.3 0.1 dynamic_slice.54
  95.4 7.5 %convolution_add_fusion.2 = f32[64,16384]{1,0:T(8,128)} fusion(f32[64,16384]{1,0:T(8,128)} %get-tuple-element.234, f32[4,8,128,128]{3,2,1,0:T(8,128)S(1)} %bitcast.64, pred[]{:T(512)S(6)} %compare.3, s32[32]{0:T(128)S(1)} %dynamic_slice.54, pred[32]{0:T(512)(128)(4,1)S(1)} %dynamic_slice.55), kind=kOutput, calls=%fused_computation.2.clone.1 | convolution fusion | flops 404754432 | bytes 10485921 | tf_op jit(solution)/shard_map/while/body/eval_jaxpr/dot_general | solution.py:54
  102.9 2.7 %fusion.36 = f32[32,128,128]{2,1,0:T(8,128)S(1)} fusion(bf16[1,384,128,128]{3,2,1,0:T(8,128)(2,1)} %get-tuple-element.248, s32[]{:T(128)S(6)} %select_n.72, bf16[1,384,128,128]{3,2,1,0:T(8,128)(2,1)} %get-tuple-element.247), kind=kOutput, calls=%fused_computation.6.clone.1 | convolution fusion | flops 268959744 | bytes 5244416 | tf_op jit(solution)/shard_map/while/body/eval_jaxpr/prc,prd->pcd/dot_general | solution.py:49
  105.6 0.1 dynamic_slice.54
  105.8 7.5 %convolution_add_fusion.2 = f32[64,16384]{1,0:T(8,128)} fusion(f32[64,16384]{1,0:T(8,128)} %get-tuple-element.234, f32[4,8,128,128]{3,2,1,0:T(8,128)S(1)} %bitcast.64, pred[]{:T(512)S(6)} %compare.3, s32[32]{0:T(128)S(1)} %dynamic_slice.54, pred[32]{0:T(512)(128)(4,1)S(1)} %dynamic_slice.55), kind=kOutput, calls=%fused_computation.2.clone.1 | convolution fusion | flops 404754432 | bytes 10485921 | tf_op jit(solution)/shard_map/while/body/eval_jaxpr/dot_general | solution.py:54
  113.3 2.6 %fusion.36 = f32[32,128,128]{2,1,0:T(8,128)S(1)} fusion(bf16[1,384,128,128]{3,2,1,0:T(8,128)(2,1)} %get-tuple-element.248, s32[]{:T(128)S(6)} %select_n.72, bf16[1,384,128,128]{3,2,1,0:T(8,128)(2,1)} %get-tuple-element.247), kind=kOutput, calls=%fused_computation.6.clone.1 | convolution fusion | flops 268959744 | bytes 5244416 | tf_op jit(solution)/shard_map/while/body/eval_jaxpr/prc,prd->pcd/dot_general | solution.py:49
  115.9 0.1 dynamic_slice.54
  116.1 7.5 %convolution_add_fusion.2 = f32[64,16384]{1,0:T(8,128)} fusion(f32[64,16384]{1,0:T(8,128)} %get-tuple-element.234, f32[4,8,128,128]{3,2,1,0:T(8,128)S(1)} %bitcast.64, pred[]{:T(512)S(6)} %compare.3, s32[32]{0:T(128)S(1)} %dynamic_slice.54, pred[32]{0:T(512)(128)(4,1)S(1)} %dynamic_slice.55), kind=kOutput, calls=%fused_computation.2.clone.1 | convolution fusion | flops 404754432 | bytes 10485921 | tf_op jit(solution)/shard_map/while/body/eval_jaxpr/dot_general | solution.py:54
  123.6 2.9 %copy.65 = f32[8,8,128,128]{3,2,1,0:T(8,128)S(1)} copy(f32[8,8,128,128]{3,1,2,0:T(8,128)} %bitcast.65) | data formatting | bytes 8388608
  126.5 3.8 %fusion.24 = (f32[64,64,64]{2,1,0:T(8,128)}, f32[64,64,64]{2,1,0:T(8,128)}, f32[64,64,64]{2,1,0:T(8,128)}) fusion(f32[64,128,128]{2,1,0:T(8,128)S(1)} %bitcast.66), kind=kLoop, calls=%fused_computation.43 | loop fusion | bytes 6291456 | tf_op jit(solution)/shard_map/slice | solution.py:68
  130.3 2.4 copy.62
  132.7 4.2 %copy.61 = f32[64,64,64]{0,1,2:T(8,128)} copy(f32[64,64,64]{2,1,0:T(8,128)} %get-tuple-element.177) | data formatting | bytes 2097152
  136.8 4.2 %copy.63 = f32[64,64,64]{0,1,2:T(8,128)} copy(f32[64,64,64]{2,1,0:T(8,128)} %get-tuple-element.178) | data formatting | bytes 2097152
  141.0 0.9 gather_fusion
  141.9 2.1 fusion.19
  144.0 0.1 copy-done
  144.1 2.4 maximum_bitcast_fusion
  146.5 6.4 %copy.53 = f32[64,1,129,64]{2,3,1,0:T(8,128)} copy(f32[64,1,129,64]{0,2,3,1:T(8,128)} %maximum_bitcast_fusion) | data formatting | bytes 4227072 | tf_op jit(solution)/shard_map/reshape | solution.py:14
  152.9 62.3 %all_to_all.5 = f32[64,1,129,64]{2,3,1,0:T(8,128)} all-to-all(f32[64,1,129,64]{2,3,1,0:T(8,128)} %copy.53), channel_id=1, replica_groups=mesh['sec_0'=4,'sec_1'=4,'sec_2'=4,'node'=2] {'sec_0','sec_1','sec_2'}, dimensions={0} | all-to-all | bytes 4227072 | tf_op jit(solution)/shard_map/all_to_all | solution.py:20
  215.2 2.5 reduce_sum.30
  217.7 0.1 slice_reduce_fusion
  217.8 0.1 copy.57
  217.9 0.1 fusion.21
  218.1 0.1 copy.55
  218.3 0.7 fusion.20
  219.0 7.3 %psum.28 = f32[]{:T(128)} all-reduce(f32[]{:T(128)} %fusion.20), channel_id=1, replica_groups=mesh['sec_0'=4,'sec_1'=4,'sec_2'=4,'node'=2] {'sec_0'}, use_global_device_ids=true, to_apply=%region_5.6 | all-reduce | flops 1 | bytes 8 | tf_op jit(solution)/shard_map/psum | solution.py:26
  226.3 10.5 %psum.29 = f32[]{:T(128)} all-reduce(f32[]{:T(128)} %psum.28), channel_id=1, replica_groups=mesh['sec_0'=4,'sec_1'=4,'sec_2'=4,'node'=2] {'sec_1'}, use_global_device_ids=true, to_apply=%region_6.7 | all-reduce | flops 1 | bytes 8 | tf_op jit(solution)/shard_map/psum | solution.py:26
  236.8 7.6 %psum.30 = f32[]{:T(128)} all-reduce(f32[]{:T(128)} %psum.29), channel_id=1, replica_groups=mesh['sec_0'=4,'sec_1'=4,'sec_2'=4,'node'=2] {'sec_2'}, use_global_device_ids=true, to_apply=%region_7.8 | all-reduce | flops 1 | bytes 8 | tf_op jit(solution)/shard_map/psum | solution.py:26
  244.4 0.1 maximum_bitcast_fusion.1
  244.5 9.3 %psum.31 = f32[]{:T(128)} all-reduce(f32[]{:T(128)} %psum.30), channel_id=1, replica_groups=mesh['sec_0'=4,'sec_1'=4,'sec_2'=4,'node'=2] {'node'}, use_global_device_ids=true, to_apply=%region_8.9 | all-reduce | flops 1 | bytes 8 | tf_op jit(solution)/shard_map/psum | solution.py:26
  254.5 0.6 maximum_multiply_fusion
  (21 shorter events, 1.0 us)
Async XLA Ops:
  141.9 2.2 copy-start
where the time goes:
time: 256 us; the launch traced here: 255 us
  matrix products  119 us (46%)
  blocking collectives  97 us (38%)
  local copies, waits for them, and re-layouts  27.1 us (11%)
  other arithmetic  10 us (4%)
    dot_general x12, matrix products, add_group(): lax.dot_general(selector, flat_terms, (((0,), (0,)), ((), ())), precision...  87.8 us
    all_to_all x1, blocking collectives, sum_at_owner(): lax.all_to_all(cut_along(shard, dim, length), axis, 0, 0, tiled=True)  62.3 us
    psum x4, blocking collectives, by_axis(): shard = lax.psum(shard, axis)  34.7 us
    dot_general x12, matrix products, add_group(): jnp.einsum('prc,prd->pcd', weights, product, preferred_element_type=jnp.f...  31.6 us
    unnamed x6, local copies, waits for them, and re-layouts  13.7 us
    reshape x1, local copies, waits for them, and re-layouts, cut_along(): shard.reshape(*shape[:dim], length, shape[dim] // length, *shape[dim + 1:])  6.38 us

commit v1 on v0

--- a/solution.py
+++ b/solution.py
@@ -23,7 +23,7 @@
 
 def by_axis(shard, axes):
     for axis in axes:
-        shard = lax.psum(shard, axis)
+        shard = jnp.sum(lax.all_gather(shard, axis), axis=0)
     return shard
 
 

time: 256 us -> 269 us (1.051)
  blocking collectives: 97 us -> 35.4 us
  waiting for transfers between devices: 0 us -> 50.7 us
  starting transfers between devices: 0 us -> 12.3 us
  local copies, waits for them, and re-layouts: 27.1 us -> 35.4 us
    all_to_all x1 -> x0, blocking collectives: 62.3 us -> none  [sum_at_owner(): lax.all_to_all(cut_along(shard, dim, length), axis, 0, 0, tiled=True)]
    all_to_all x0 -> x1, waiting for transfers between devices: none -> 50.7 us  [sum_at_owner(): lax.all_to_all(cut_along(shard, dim, length), axis, 0, 0, tiled=True)]
    unnamed x0 -> x4, blocking collectives: none -> 35.4 us
    psum x4 -> x0, blocking collectives: 34.7 us -> none  [by_axis(): shard = lax.psum(shard, axis)]
    all_to_all x0 -> x1, starting transfers between devices: none -> 12.3 us  [sum_at_owner(): lax.all_to_all(cut_along(shard, dim, length), axis, 0, 0, tiled=True)]
    unnamed x6 -> x26, local copies, waits for them, and re-layouts: 13.7 us -> 22 us
  transfers between devices with their start and end apart: 0 -> 1, of which waited for: 0 -> 1; matrix products, arithmetic and copies ran while one was open for 0% -> 0% of each run, Pallas kernels for 0% -> 0%
where the time goes in v1:
time: 269 us; the launch traced here: 267 us
  matrix products  119 us (44%)
  waiting for transfers between devices  50.7 us (19%)
  local copies, waits for them, and re-layouts  35.4 us (13%)
  blocking collectives  35.4 us (13%)
  other arithmetic  12.4 us (5%)
  starting transfers between devices  12.3 us (5%)
    dot_general x12, matrix products, add_group(): lax.dot_general(selector, flat_terms, (((0,), (0,)), ((), ())), precision...  87.8 us
    all_to_all x1, waiting for transfers between devices, sum_at_owner(): lax.all_to_all(cut_along(shard, dim, length), axis, 0, 0, tiled=True)  50.7 us
    unnamed x4, blocking collectives  35.4 us
    dot_general x12, matrix products, add_group(): jnp.einsum('prc,prd->pcd', weights, product, preferred_element_type=jnp.f...  31.6 us
    unnamed x26, local copies, waits for them, and re-layouts  22 us
    all_to_all x1, starting transfers between devices, sum_at_owner(): lax.all_to_all(cut_along(shard, dim, length), axis, 0, 0, tiled=True)  12.3 us
    reshape x1, local copies, waits for them, and re-layouts, cut_along(): shard.reshape(*shape[:dim], length, shape[dim] // length, *shape[dim + 1:])  6.38 us
  transfers between devices with their start and end apart: 1, of which 1 were waited for; matrix products, arithmetic and copies ran while one was open for 0% of the time, Pallas kernels for 0%

profile of v1, /device:TPU:1, one launch (start us, length us, event | category | flops | bytes accessed | tf_op | source)
XLA Modules:
  0.0 267.4 jit_solution(6140445280505164742)
XLA Ops:
  0.0 0.7 reduce.5
  1.4 0.7 select_reduce_fusion
  2.1 121.4 %while.14 = (s32[]{:T(128)}, f32[64,16384]{1,0:T(8,128)}, s32[384]{0:T(512)S(1)}, pred[384]{0:T(512)(128)(4,1)S(1)}, bf16[1,384,128,128]{3,2,1,0:T(8,128)(2,1)},...) while((s32[]{:T(128)}, f32[64,16384]{1,0:T(8,128)}, ...), condition=%wide.region_2.3_spmd.clone, body=%wide.region_1.2_spmd.clone.sunk | while | flops 673714176 | bytes 15730821 | solution.py:65
  2.1 2.6 fusion.36
  4.8 0.1 dynamic_slice.54
  4.9 5.3 %convolution_add_fusion.2 = f32[64,16384]{1,0:T(8,128)} fusion(f32[64,16384]{1,0:T(8,128)} %get-tuple-element.234, f32[4,8,128,128]{3,2,1,0:T(8,128)S(1)} %bitcast.72, pred[]{:T(512)S(6)} %compare.3, s32[32]{0:T(128)S(1)} %dynamic_slice.54, pred[32]{0:T(512)(128)(4,1)S(1)} %dynamic_slice.55), kind=kOutput, calls=%fused_computation.2.clone.1 | convolution fusion | flops 404754432 | bytes 10485921 | tf_op jit(solution)/shard_map/while/body/eval_jaxpr/dot_general | solution.py:54
  10.2 2.6 fusion.36
  13.0 7.5 %convolution_add_fusion.2 = f32[64,16384]{1,0:T(8,128)} fusion(f32[64,16384]{1,0:T(8,128)} %get-tuple-element.234, f32[4,8,128,128]{3,2,1,0:T(8,128)S(1)} %bitcast.72, pred[]{:T(512)S(6)} %compare.3, s32[32]{0:T(128)S(1)} %dynamic_slice.54, pred[32]{0:T(512)(128)(4,1)S(1)} %dynamic_slice.55), kind=kOutput, calls=%fused_computation.2.clone.1 | convolution fusion | flops 404754432 | bytes 10485921 | tf_op jit(solution)/shard_map/while/body/eval_jaxpr/dot_general | solution.py:54
  20.5 2.6 fusion.36
  23.3 7.5 %convolution_add_fusion.2 = f32[64,16384]{1,0:T(8,128)} fusion(f32[64,16384]{1,0:T(8,128)} %get-tuple-element.234, f32[4,8,128,128]{3,2,1,0:T(8,128)S(1)} %bitcast.72, pred[]{:T(512)S(6)} %compare.3, s32[32]{0:T(128)S(1)} %dynamic_slice.54, pred[32]{0:T(512)(128)(4,1)S(1)} %dynamic_slice.55), kind=kOutput, calls=%fused_computation.2.clone.1 | convolution fusion | flops 404754432 | bytes 10485921 | tf_op jit(solution)/shard_map/while/body/eval_jaxpr/dot_general | solution.py:54
  30.8 2.6 fusion.36
  33.5 7.5 %convolution_add_fusion.2 = f32[64,16384]{1,0:T(8,128)} fusion(f32[64,16384]{1,0:T(8,128)} %get-tuple-element.234, f32[4,8,128,128]{3,2,1,0:T(8,128)S(1)} %bitcast.72, pred[]{:T(512)S(6)} %compare.3, s32[32]{0:T(128)S(1)} %dynamic_slice.54, pred[32]{0:T(512)(128)(4,1)S(1)} %dynamic_slice.55), kind=kOutput, calls=%fused_computation.2.clone.1 | convolution fusion | flops 404754432 | bytes 10485921 | tf_op jit(solution)/shard_map/while/body/eval_jaxpr/dot_general | solution.py:54
  41.0 2.6 fusion.36
  43.8 7.5 %convolution_add_fusion.2 = f32[64,16384]{1,0:T(8,128)} fusion(f32[64,16384]{1,0:T(8,128)} %get-tuple-element.234, f32[4,8,128,128]{3,2,1,0:T(8,128)S(1)} %bitcast.72, pred[]{:T(512)S(6)} %compare.3, s32[32]{0:T(128)S(1)} %dynamic_slice.54, pred[32]{0:T(512)(128)(4,1)S(1)} %dynamic_slice.55), kind=kOutput, calls=%fused_computation.2.clone.1 | convolution fusion | flops 404754432 | bytes 10485921 | tf_op jit(solution)/shard_map/while/body/eval_jaxpr/dot_general | solution.py:54
  51.3 2.6 fusion.36
  54.1 7.5 %convolution_add_fusion.2 = f32[64,16384]{1,0:T(8,128)} fusion(f32[64,16384]{1,0:T(8,128)} %get-tuple-element.234, f32[4,8,128,128]{3,2,1,0:T(8,128)S(1)} %bitcast.72, pred[]{:T(512)S(6)} %compare.3, s32[32]{0:T(128)S(1)} %dynamic_slice.54, pred[32]{0:T(512)(128)(4,1)S(1)} %dynamic_slice.55), kind=kOutput, calls=%fused_computation.2.clone.1 | convolution fusion | flops 404754432 | bytes 10485921 | tf_op jit(solution)/shard_map/while/body/eval_jaxpr/dot_general | solution.py:54
  61.6 2.8 %fusion.36 = f32[32,128,128]{2,1,0:T(8,128)S(1)} fusion(bf16[1,384,128,128]{3,2,1,0:T(8,128)(2,1)} %get-tuple-element.248, s32[]{:T(128)S(6)} %select_n.72, bf16[1,384,128,128]{3,2,1,0:T(8,128)(2,1)} %get-tuple-element.247), kind=kOutput, calls=%fused_computation.6.clone.1 | convolution fusion | flops 268959744 | bytes 5244416 | tf_op jit(solution)/shard_map/while/body/eval_jaxpr/prc,prd->pcd/dot_general | solution.py:49
  64.6 7.5 %convolution_add_fusion.2 = f32[64,16384]{1,0:T(8,128)} fusion(f32[64,16384]{1,0:T(8,128)} %get-tuple-element.234, f32[4,8,128,128]{3,2,1,0:T(8,128)S(1)} %bitcast.72, pred[]{:T(512)S(6)} %compare.3, s32[32]{0:T(128)S(1)} %dynamic_slice.54, pred[32]{0:T(512)(128)(4,1)S(1)} %dynamic_slice.55), kind=kOutput, calls=%fused_computation.2.clone.1 | convolution fusion | flops 404754432 | bytes 10485921 | tf_op jit(solution)/shard_map/while/body/eval_jaxpr/dot_general | solution.py:54
  72.1 2.6 fusion.36
  74.9 7.5 %convolution_add_fusion.2 = f32[64,16384]{1,0:T(8,128)} fusion(f32[64,16384]{1,0:T(8,128)} %get-tuple-element.234, f32[4,8,128,128]{3,2,1,0:T(8,128)S(1)} %bitcast.72, pred[]{:T(512)S(6)} %compare.3, s32[32]{0:T(128)S(1)} %dynamic_slice.54, pred[32]{0:T(512)(128)(4,1)S(1)} %dynamic_slice.55), kind=kOutput, calls=%fused_computation.2.clone.1 | convolution fusion | flops 404754432 | bytes 10485921 | tf_op jit(solution)/shard_map/while/body/eval_jaxpr/dot_general | solution.py:54
  82.4 2.6 fusion.36
  85.2 7.5 %convolution_add_fusion.2 = f32[64,16384]{1,0:T(8,128)} fusion(f32[64,16384]{1,0:T(8,128)} %get-tuple-element.234, f32[4,8,128,128]{3,2,1,0:T(8,128)S(1)} %bitcast.72, pred[]{:T(512)S(6)} %compare.3, s32[32]{0:T(128)S(1)} %dynamic_slice.54, pred[32]{0:T(512)(128)(4,1)S(1)} %dynamic_slice.55), kind=kOutput, calls=%fused_computation.2.clone.1 | convolution fusion | flops 404754432 | bytes 10485921 | tf_op jit(solution)/shard_map/while/body/eval_jaxpr/dot_general | solution.py:54
  92.7 2.6 fusion.36
  95.4 7.5 %convolution_add_fusion.2 = f32[64,16384]{1,0:T(8,128)} fusion(f32[64,16384]{1,0:T(8,128)} %get-tuple-element.234, f32[4,8,128,128]{3,2,1,0:T(8,128)S(1)} %bitcast.72, pred[]{:T(512)S(6)} %compare.3, s32[32]{0:T(128)S(1)} %dynamic_slice.54, pred[32]{0:T(512)(128)(4,1)S(1)} %dynamic_slice.55), kind=kOutput, calls=%fused_computation.2.clone.1 | convolution fusion | flops 404754432 | bytes 10485921 | tf_op jit(solution)/shard_map/while/body/eval_jaxpr/dot_general | solution.py:54
  102.9 2.7 fusion.36
  105.8 7.5 %convolution_add_fusion.2 = f32[64,16384]{1,0:T(8,128)} fusion(f32[64,16384]{1,0:T(8,128)} %get-tuple-element.234, f32[4,8,128,128]{3,2,1,0:T(8,128)S(1)} %bitcast.72, pred[]{:T(512)S(6)} %compare.3, s32[32]{0:T(128)S(1)} %dynamic_slice.54, pred[32]{0:T(512)(128)(4,1)S(1)} %dynamic_slice.55), kind=kOutput, calls=%fused_computation.2.clone.1 | convolution fusion | flops 404754432 | bytes 10485921 | tf_op jit(solution)/shard_map/while/body/eval_jaxpr/dot_general | solution.py:54
  113.3 2.6 fusion.36
  116.1 7.5 %convolution_add_fusion.2 = f32[64,16384]{1,0:T(8,128)} fusion(f32[64,16384]{1,0:T(8,128)} %get-tuple-element.234, f32[4,8,128,128]{3,2,1,0:T(8,128)S(1)} %bitcast.72, pred[]{:T(512)S(6)} %compare.3, s32[32]{0:T(128)S(1)} %dynamic_slice.54, pred[32]{0:T(512)(128)(4,1)S(1)} %dynamic_slice.55), kind=kOutput, calls=%fused_computation.2.clone.1 | convolution fusion | flops 404754432 | bytes 10485921 | tf_op jit(solution)/shard_map/while/body/eval_jaxpr/dot_general | solution.py:54
  123.6 2.9 %copy.65 = f32[8,8,128,128]{3,2,1,0:T(8,128)S(1)} copy(f32[8,8,128,128]{3,1,2,0:T(8,128)} %bitcast.73) | data formatting | bytes 8388608
  126.5 3.8 %fusion.24 = (f32[64,64,64]{2,1,0:T(8,128)}, f32[64,64,64]{2,1,0:T(8,128)}, f32[64,64,64]{2,1,0:T(8,128)}) fusion(f32[64,128,128]{2,1,0:T(8,128)S(1)} %bitcast.74), kind=kLoop, calls=%fused_computation.43 | loop fusion | bytes 6291456 | tf_op jit(solution)/shard_map/slice | solution.py:68
  130.3 2.4 copy.62
  132.7 4.2 %copy.61 = f32[64,64,64]{0,1,2:T(8,128)} copy(f32[64,64,64]{2,1,0:T(8,128)} %get-tuple-element.177) | data formatting | bytes 2097152
  136.8 4.2 %copy.63 = f32[64,64,64]{0,1,2:T(8,128)} copy(f32[64,64,64]{2,1,0:T(8,128)} %get-tuple-element.178) | data formatting | bytes 2097152
  141.0 0.9 gather_fusion
  141.9 2.1 fusion.19
  144.0 0.1 copy-done
  144.1 2.4 maximum_bitcast_fusion
  146.5 6.4 %copy.53 = f32[64,1,129,64]{2,3,1,0:T(8,128)} copy(f32[64,1,129,64]{0,2,3,1:T(8,128)} %maximum_bitcast_fusion) | data formatting | bytes 4227072 | tf_op jit(solution)/shard_map/reshape | solution.py:14
  152.9 12.3 %all-to-all-start = ((f32[64,1,129,64]{2,3,1,0:T(8,128)}), f32[64,1,129,64]{2,3,1,0:T(8,128)}, u32[]{:S(2)}, u32[]{:S(2)}) async-start(f32[64,1,129,64]{2,3,1,0:T(8,128)} %copy.53), calls=%async_computation | async-start | bytes 8388608 | tf_op jit(solution)/shard_map/all_to_all | solution.py:20
  165.3 0.6 dynamic-slice.6
  165.9 50.7 %all-to-all-done = f32[64,1,129,64]{2,3,1,0:T(8,128)} async-done(((f32[64,1,129,64]{2,3,1,0:T(8,128)}), f32[64,1,129,64]{2,3,1,0:T(8,128)}, u32[]{:S(2)}, u32[]{:S(2)}) %all-to-all-start) | async-done | bytes 2113568 | tf_op jit(solution)/shard_map/all_to_all | solution.py:20
  216.6 2.5 reduce_sum.66
  219.1 0.1 slice_reduce_fusion
  219.3 0.1 copy.57
  219.3 0.1 fusion.21
  219.5 0.1 copy.55
  219.7 0.7 fusion.20
  220.4 1.4 dynamic-update-slice
  221.8 0.7 dynamic-slice.7
  222.4 9.2 %all-reduce = f32[4]{0:T(128)S(1)} all-reduce(f32[4]{0:T(128)S(1)} %dynamic-update-slice), channel_id=1, replica_groups=mesh['sec_0'=4,'sec_1'=4,'sec_2'=4,'node'=2] {'sec_0'}, use_global_device_ids=true, to_apply=%add | all-reduce | flops 4 | bytes 32
  231.6 0.6 reduce_sum.69
  232.2 1.4 dynamic-update-slice.1
  233.7 0.7 dynamic-slice.8
  234.3 9.3 %all-reduce.1 = f32[4]{0:T(128)S(1)} all-reduce(f32[4]{0:T(128)S(1)} %dynamic-update-slice.1), channel_id=1, replica_groups=mesh['sec_0'=4,'sec_1'=4,'sec_2'=4,'node'=2] {'sec_1'}, use_global_device_ids=true, to_apply=%add.1 | all-reduce | flops 4 | bytes 32
  243.7 0.6 reduce_sum.70
  244.3 1.4 dynamic-update-slice.2
  245.7 0.7 dynamic-slice.9
  246.4 7.0 %all-reduce.2 = f32[4]{0:T(128)S(1)} all-reduce(f32[4]{0:T(128)S(1)} %dynamic-update-slice.2), channel_id=1, replica_groups=mesh['sec_0'=4,'sec_1'=4,'sec_2'=4,'node'=2] {'sec_2'}, use_global_device_ids=true, to_apply=%add.2 | all-reduce | flops 4 | bytes 32
  253.4 0.6 reduce_sum.71
  254.0 1.4 dynamic-update-slice.3
  255.4 0.1 maximum_bitcast_fusion.1
  255.5 9.9 %all-reduce.3 = f32[2]{0:T(128)S(1)} all-reduce(f32[2]{0:T(128)S(1)} %dynamic-update-slice.3), channel_id=1, replica_groups=mesh['sec_0'=4,'sec_1'=4,'sec_2'=4,'node'=2] {'node'}, use_global_device_ids=true, to_apply=%add.3 | all-reduce | flops 2 | bytes 16
  265.4 0.6 reduce_sum.72
  266.7 0.6 maximum_multiply_fusion
  (46 shorter events, 2.1 us)
Async XLA Ops:
  141.9 2.2 copy-start
  152.9 12.4 %copy-start.4 = (u32[128]{0:T(128)S(1)}, u32[128]{0:T(128)}, u32[]{:S(2)}) copy-start(u32[128]{0:T(128)} %constant.91) | copy-start | bytes 1540
  152.9 63.7 %all-to-all-start = ((f32[64,1,129,64]{2,3,1,0:T(8,128)}), f32[64,1,129,64]{2,3,1,0:T(8,128)}, u32[]{:S(2)}, u32[]{:S(2)}) async-start(f32[64,1,129,64]{2,3,1,0:T(8,128)} %copy.53), calls=%async_computation | async-start | bytes 8388608 | tf_op jit(solution)/shard_map/all_to_all | solution.py:20
  165.2 56.5 %copy-start.3 = (u32[128]{0:T(128)S(1)}, u32[128]{0:T(128)}, u32[]{:S(2)}) copy-start(u32[128]{0:T(128)} %constant.96) | copy-start | bytes 1540
  165.2 68.4 %copy-start.2 = (u32[128]{0:T(128)S(1)}, u32[128]{0:T(128)}, u32[]{:S(2)}) copy-start(u32[128]{0:T(128)} %constant.101) | copy-start | bytes 1540
  165.3 80.5 %copy-start.1 = (u32[128]{0:T(128)S(1)}, u32[128]{0:T(128)}, u32[]{:S(2)}) copy-start(u32[128]{0:T(128)} %constant.106) | copy-start | bytes 1540
